TPU v7x, 32 devices: a whole 2x2x4 slice. The times are simulated.
32 devices in a mesh: patch: 16 (over z, y, x), col: 2 (over core).
Axes of the slice: x: 2, y: 2, z: 4, core: 2. Of those that a mesh axis runs over, the one named last changes fastest.
Arguments:
- density: float32 [4, 16384], P(None, 'patch'), may hold values from -6 to 6
- block_values: bfloat16 [64, 32, 256, 256], P('patch', 'col'), may hold values from -0.09375 to 0.09375
- block_rows: int32 [64, 32], P('patch', 'col'), may hold values from 0 to 63, as said below
- block_counts: int32 [64], P('patch'), may hold values from 1 to 32
Outputs:
- potential: float32 [4, 16384], P(None, 'patch')
Inputs may be any that keep to these rules, and one draw needn't show every extreme that they name: `block_rows`: slots of a block column at or past its count are padding and are not part of the matrix. Block row r belongs to owner r // 4. The slots held by one device (block columns of one patch owner, one col index, live or padding) name block rows of distinct owners in groups of exactly 8 slots a group, so at most 8 of them fall on one owner.
All inputs are finite; a program needn't handle non-finite values.
Results may differ from a plain program's by a relative error of at most 0.0027.
Values sent between devices are 32-bit elements; how exact they have to be, the bound alone decides.
A program may use at most 64 MiB of HBM per device.

v0:
```python
import jax
import jax.numpy as jnp
from jax import lax
from jax.sharding import PartitionSpec as P

LEVELS = 3


def passed_along(block, axis, distance):
    devices = range(lax.axis_size(axis))
    route = [(i - distance, i) for i in devices if i - distance in devices]
    return lax.ppermute(block, axis, route)


def body(density, block_values, block_rows, block_counts):
    sides = density.shape[0]
    col_blocks = block_values.shape[0]
    slots = block_values.shape[1]
    block = block_values.shape[2]
    local_len = density.shape[1]
    details = []
    smooth = density
    for level_index in range(LEVELS):
        even_part = smooth[:, 0::2]
        odd_part = smooth[:, 1::2]
        arriving = passed_along(even_part[:, :1], "patch", -1)
        even_next = jnp.concatenate([even_part[:, 1:], arriving], axis=1)
        detail = odd_part - 0.5 * (even_part + even_next)
        leaving = passed_along(detail[:, -1:], "patch", 1)
        detail_prior = jnp.concatenate([leaving, detail[:, :-1]], axis=1)
        smooth = even_part + 0.25 * (detail_prior + detail)
        details.append(detail)
    vector = jnp.concatenate([smooth] + details[::-1], axis=1).astype(jnp.bfloat16)
    blocks = vector.reshape(sides, col_blocks, block).transpose(1, 0, 2)
    terms = jnp.einsum("cjkm,crm->cjrk", block_values, blocks, preferred_element_type=jnp.float32)
    first_slot = lax.axis_index("col") * slots
    live = first_slot + jnp.arange(slots, dtype=jnp.int32)[None, :] < block_counts[:, None]
    owners = lax.axis_size("patch")
    row_blocks = owners * col_blocks
    width = sides * block
    hits = (
        block_rows.reshape(1, -1) == jnp.arange(row_blocks, dtype=jnp.int32)[:, None]
    ) & live.reshape(1, -1)
    partial_value = jnp.dot(
        hits.astype(jnp.float32), terms.reshape(-1, width), precision=lax.Precision.HIGHEST
    )
    arrived = lax.all_to_all(
        partial_value.reshape(owners, col_blocks, width),
        "patch",
        split_axis=0,
        concat_axis=0,
        tiled=True,
    )
    summed = lax.psum(jnp.sum(arrived, axis=0), "col")
    local = summed.reshape(col_blocks, sides, block).transpose(1, 0, 2).reshape(sides, local_len)
    coarse = local_len // 2**LEVELS
    smooth = local[:, :coarse]
    for level_index in range(LEVELS, 0, -1):
        lower = local_len // 2**level_index
        upper = local_len // 2 ** (level_index - 1)
        detail = local[:, lower:upper]
        leaving = passed_along(detail[:, -1:], "patch", 1)
        detail_prior = jnp.concatenate([leaving, detail[:, :-1]], axis=1)
        even_part = smooth - 0.25 * (detail_prior + detail)
        arriving = passed_along(even_part[:, :1], "patch", -1)
        even_next = jnp.concatenate([even_part[:, 1:], arriving], axis=1)
        odd_part = detail + 0.5 * (even_part + even_next)
        smooth = jnp.stack([even_part, odd_part], axis=-1).reshape(sides, -1)
    return 0.5 * density + smooth


def solution(mesh):
    return jax.shard_map(
        body,
        mesh=mesh,
        in_specs=(P(None, "patch"), P("patch", "col", None, None), P("patch", "col"), P("patch")),
        out_specs=P(None, "patch"),
        check_vma=False,
    )
```

profile of v0, /device:TPU:6, one launch (start us, length us, event | category | flops | bytes accessed | tf_op | source)
XLA Modules:
  0.0 100.5 jit_solution(5695332042901219780)
XLA Ops:
  0.0 1.1 %slice.108 = f32[4,512]{1,0:T(4,128)S(1)} slice(f32[4,1024]{1,0:T(4,128)} %param.4), slice={[0:4:1], [0:1024:2]} | slice | bytes 16384 | tf_op jit(solution)/shard_map/slice | solution.py:24
  1.1 2.4 %collective-permute-start = (f32[4,1]{1,0:T(4,128)S(1)}, f32[4,1]{1,0:T(4,128)S(1)}, u32[]{:S(2)}, u32[]{:S(2)}) collective-permute-start(f32[4,1]{1,0:T(4,128)S(1)} %slice.143), channel_id=1, source_target_pairs={{2,0},{4,2},{6,4},{8,6},{10,8},{12,10},{14,12},{16,14},{18,16},{20... | collective-permute-start | bytes 56 | tf_op jit(solution)/shard_map/ppermute | solution.py:12
  3.7 1.1 %slice.109 = f32[4,512]{1,0:T(4,128)S(1)} slice(f32[4,1024]{1,0:T(4,128)} %param.4), slice={[0:4:1], [1:1024:2]} | slice | bytes 16384 | tf_op jit(solution)/shard_map/slice | solution.py:25
  4.8 0.7 broadcast_compare_fusion
  5.5 0.1 lt.23
  5.6 0.8 eq.26
  6.4 2.1 %collective-permute-done = f32[4,1]{1,0:T(4,128)S(1)} collective-permute-done((f32[4,1]{1,0:T(4,128)S(1)}, f32[4,1]{1,0:T(4,128)S(1)}, u32[]{:S(2)}, u32[]{:S(2)}) %collective-permute-start) | collective-permute-done | bytes 48 | tf_op jit(solution)/shard_map/ppermute | solution.py:12
  8.4 0.1 fusion.37
  8.6 3.1 %collective-permute-start.1 = (f32[4,1]{1,0:T(4,128)S(1)}, f32[4,1]{1,0:T(4,128)S(1)}, u32[]{:S(2)}, u32[]{:S(2)}) collective-permute-start(f32[4,1]{1,0:T(4,128)S(1)} %slice.144), channel_id=1, source_target_pairs={{0,2},{2,4},{4,6},{6,8},{8,10},{10,12},{12,14},{14,16},{16,18},{18... | collective-permute-start | bytes 56 | tf_op jit(solution)/shard_map/ppermute | solution.py:12
  11.7 2.3 %collective-permute-done.1 = f32[4,1]{1,0:T(4,128)S(1)} collective-permute-done((f32[4,1]{1,0:T(4,128)S(1)}, f32[4,1]{1,0:T(4,128)S(1)}, u32[]{:S(2)}, u32[]{:S(2)}) %collective-permute-start.1) | collective-permute-done | bytes 48 | tf_op jit(solution)/shard_map/ppermute | solution.py:12
  14.1 0.2 slice.114
  14.3 0.2 slice.115
  14.7 2.2 %collective-permute-start.2 = (f32[4,1]{1,0:T(4,128)S(1)}, f32[4,1]{1,0:T(4,128)S(1)}, u32[]{:S(2)}, u32[]{:S(2)}) collective-permute-start(f32[4,1]{1,0:T(4,128)S(1)} %slice.147), channel_id=1, source_target_pairs={{2,0},{4,2},{6,4},{8,6},{10,8},{12,10},{14,12},{16,14},{18,16},{20... | collective-permute-start | bytes 56 | tf_op jit(solution)/shard_map/ppermute | solution.py:12
  16.8 5.1 %collective-permute-done.2 = f32[4,1]{1,0:T(4,128)S(1)} collective-permute-done((f32[4,1]{1,0:T(4,128)S(1)}, f32[4,1]{1,0:T(4,128)S(1)}, u32[]{:S(2)}, u32[]{:S(2)}) %collective-permute-start.2) | collective-permute-done | bytes 48 | tf_op jit(solution)/shard_map/ppermute | solution.py:12
  21.9 0.1 fusion.35
  22.1 3.1 %collective-permute-start.3 = (f32[4,1]{1,0:T(4,128)S(1)}, f32[4,1]{1,0:T(4,128)S(1)}, u32[]{:S(2)}, u32[]{:S(2)}) collective-permute-start(f32[4,1]{1,0:T(4,128)S(1)} %slice.148), channel_id=1, source_target_pairs={{0,2},{2,4},{4,6},{6,8},{8,10},{10,12},{12,14},{14,16},{16,18},{18... | collective-permute-start | bytes 56 | tf_op jit(solution)/shard_map/ppermute | solution.py:12
  25.2 2.3 %collective-permute-done.3 = f32[4,1]{1,0:T(4,128)S(1)} collective-permute-done((f32[4,1]{1,0:T(4,128)S(1)}, f32[4,1]{1,0:T(4,128)S(1)}, u32[]{:S(2)}, u32[]{:S(2)}) %collective-permute-start.3) | collective-permute-done | bytes 48 | tf_op jit(solution)/shard_map/ppermute | solution.py:12
  27.6 0.2 slice.120
  27.8 0.2 slice.121
  28.1 1.9 %collective-permute-start.4 = (f32[4,1]{1,0:T(4,128)S(1)}, f32[4,1]{1,0:T(4,128)S(1)}, u32[]{:S(2)}, u32[]{:S(2)}) collective-permute-start(f32[4,1]{1,0:T(4,128)S(1)} %bitcast.43), channel_id=1, source_target_pairs={{2,0},{4,2},{6,4},{8,6},{10,8},{12,10},{14,12},{16,14},{18,16},{20... | collective-permute-start | bytes 56 | tf_op jit(solution)/shard_map/ppermute | solution.py:12
  30.1 5.3 %collective-permute-done.4 = f32[4,1]{1,0:T(4,128)S(1)} collective-permute-done((f32[4,1]{1,0:T(4,128)S(1)}, f32[4,1]{1,0:T(4,128)S(1)}, u32[]{:S(2)}, u32[]{:S(2)}) %collective-permute-start.4) | collective-permute-done | bytes 48 | tf_op jit(solution)/shard_map/ppermute | solution.py:12
  35.4 0.1 fusion.33
  35.6 3.1 %collective-permute-start.5 = (f32[4,1]{1,0:T(4,128)S(1)}, f32[4,1]{1,0:T(4,128)S(1)}, u32[]{:S(2)}, u32[]{:S(2)}) collective-permute-start(f32[4,1]{1,0:T(4,128)S(1)} %slice.124), channel_id=1, source_target_pairs={{0,2},{2,4},{4,6},{6,8},{8,10},{10,12},{12,14},{14,16},{16,18},{18... | collective-permute-start | bytes 56 | tf_op jit(solution)/shard_map/ppermute | solution.py:12
  38.7 2.3 %collective-permute-done.5 = f32[4,1]{1,0:T(4,128)S(1)} collective-permute-done((f32[4,1]{1,0:T(4,128)S(1)}, f32[4,1]{1,0:T(4,128)S(1)}, u32[]{:S(2)}, u32[]{:S(2)}) %collective-permute-start.5) | collective-permute-done | bytes 48 | tf_op jit(solution)/shard_map/ppermute | solution.py:12
  41.1 5.6 %convolution_bitcast_fusion = f32[4,16,4,256]{3,2,1,0:T(4,128)S(1)} fusion(bf16[4,4,256,1]{2,1,3,0:T(4,128)(2,1)S(1)} %bitcast.40, bf16[4,16,256,256]{3,2,1,0:T(8,128)(2,1)} %param.5), kind=kOutput, calls=%fused_computation | convolution fusion | flops 33554432 | bytes 8658944 | tf_op jit(solution)/shard_map/cjkm,crm->cjrk/dot_general | solution.py:35
  46.8 0.2 reshape.76
  46.9 0.3 fusion
  47.2 0.2 copy.96
  47.4 13.1 %all_to_all.5 = f32[16,4,1024]{2,1,0:T(4,128)S(1)} all-to-all(f32[16,4,1024]{2,1,0:T(4,128)S(1)} %copy.96), channel_id=1, replica_groups=mesh['patch'=16,'col'=2] {'patch'}, dimensions={0} | all-to-all | bytes 524288 | tf_op jit(solution)/shard_map/all_to_all | solution.py:47
  60.6 3.4 %psum.7 = f32[4,1024]{1,0:T(4,128)S(1)} all-reduce(f32[4,1024]{1,0:T(4,128)S(1)} %bitcast.38), channel_id=1, replica_groups=mesh['patch'=16,'col'=2] {'col'}, use_global_device_ids=true, to_apply=%region_1.0 | all-reduce | flops 4096 | bytes 32768 | tf_op jit(solution)/shard_map/psum | solution.py:54
  64.1 4.3 %collective-permute-start.10 = (f32[4,1]{1,0:T(4,128)S(1)}, f32[4,1]{1,0:T(4,128)S(1)}, u32[]{:S(2)}, u32[]{:S(2)}) collective-permute-start(f32[4,1]{1,0:T(4,128)S(1)} %get-tuple-element.11), channel_id=1, source_target_pairs={{0,2},{2,4},{4,6},{6,8},{8,10},{10,12},{12,14},{14,16},{16,18},{18... | collective-permute-start | bytes 56 | tf_op jit(solution)/shard_map/ppermute | solution.py:12
  68.3 2.5 %collective-permute-start.8 = (f32[4,1]{1,0:T(4,128)S(1)}, f32[4,1]{1,0:T(4,128)S(1)}, u32[]{:S(2)}, u32[]{:S(2)}) collective-permute-start(f32[4,1]{1,0:T(4,128)S(1)} %get-tuple-element.12), channel_id=1, source_target_pairs={{0,2},{2,4},{4,6},{6,8},{8,10},{10,12},{12,14},{14,16},{16,18},{18... | collective-permute-start | bytes 56 | tf_op jit(solution)/shard_map/ppermute | solution.py:12
  70.8 3.9 %collective-permute-start.6 = (f32[4,1]{1,0:T(4,128)S(1)}, f32[4,1]{1,0:T(4,128)S(1)}, u32[]{:S(2)}, u32[]{:S(2)}) collective-permute-start(f32[4,1]{1,0:T(4,128)S(1)} %get-tuple-element.13), channel_id=1, source_target_pairs={{0,2},{2,4},{4,6},{6,8},{8,10},{10,12},{12,14},{14,16},{16,18},{18... | collective-permute-start | bytes 56 | tf_op jit(solution)/shard_map/ppermute | solution.py:12
  74.7 1.6 %collective-permute-done.6 = f32[4,1]{1,0:T(4,128)S(1)} collective-permute-done((f32[4,1]{1,0:T(4,128)S(1)}, f32[4,1]{1,0:T(4,128)S(1)}, u32[]{:S(2)}, u32[]{:S(2)}) %collective-permute-start.6) | collective-permute-done | bytes 48 | tf_op jit(solution)/shard_map/ppermute | solution.py:12
  76.4 4.3 %collective-permute-start.7 = (f32[4,1]{1,0:T(4,128)S(1)}, f32[4,1]{1,0:T(4,128)S(1)}, u32[]{:S(2)}, u32[]{:S(2)}) collective-permute-start(f32[4,1]{1,0:T(4,128)S(1)} %bitcast.41), channel_id=1, source_target_pairs={{2,0},{4,2},{6,4},{8,6},{10,8},{12,10},{14,12},{16,14},{18,16},{20... | collective-permute-start | bytes 56 | tf_op jit(solution)/shard_map/ppermute | solution.py:12
  80.7 3.0 %collective-permute-done.7 = f32[4,1]{1,0:T(4,128)S(1)} collective-permute-done((f32[4,1]{1,0:T(4,128)S(1)}, f32[4,1]{1,0:T(4,128)S(1)}, u32[]{:S(2)}, u32[]{:S(2)}) %collective-permute-start.7) | collective-permute-done | bytes 48 | tf_op jit(solution)/shard_map/ppermute | solution.py:12
  83.8 0.2 copy.97
  84.0 0.1 fusion.20
  84.2 2.5 %collective-permute-start.9 = (f32[4,1]{1,0:T(4,128)S(1)}, f32[4,1]{1,0:T(4,128)S(1)}, u32[]{:S(2)}, u32[]{:S(2)}) collective-permute-start(f32[4,1]{1,0:T(4,128)S(1)} %slice.158), channel_id=1, source_target_pairs={{2,0},{4,2},{6,4},{8,6},{10,8},{12,10},{14,12},{16,14},{18,16},{20... | collective-permute-start | bytes 56 | tf_op jit(solution)/shard_map/ppermute | solution.py:12
  86.7 4.8 %collective-permute-done.9 = f32[4,1]{1,0:T(4,128)S(1)} collective-permute-done((f32[4,1]{1,0:T(4,128)S(1)}, f32[4,1]{1,0:T(4,128)S(1)}, u32[]{:S(2)}, u32[]{:S(2)}) %collective-permute-start.9) | collective-permute-done | bytes 48 | tf_op jit(solution)/shard_map/ppermute | solution.py:12
  91.6 0.2 copy.99
  91.7 0.1 copy.100
  91.9 0.1 fusion.11
  92.0 1.9 %collective-permute-start.11 = (f32[4,1]{1,0:T(4,128)S(1)}, f32[4,1]{1,0:T(4,128)S(1)}, u32[]{:S(2)}, u32[]{:S(2)}) collective-permute-start(f32[4,1]{1,0:T(4,128)S(1)} %slice.163), channel_id=1, source_target_pairs={{2,0},{4,2},{6,4},{8,6},{10,8},{12,10},{14,12},{16,14},{18,16},{20... | collective-permute-start | bytes 56 | tf_op jit(solution)/shard_map/ppermute | solution.py:12
  93.9 5.3 %collective-permute-done.11 = f32[4,1]{1,0:T(4,128)S(1)} collective-permute-done((f32[4,1]{1,0:T(4,128)S(1)}, f32[4,1]{1,0:T(4,128)S(1)}, u32[]{:S(2)}, u32[]{:S(2)}) %collective-permute-start.11) | collective-permute-done | bytes 48 | tf_op jit(solution)/shard_map/ppermute | solution.py:12
  99.4 0.3 copy.101
  99.6 0.2 copy.102
  99.8 0.6 multiply_add_fusion
  (37 shorter events, 1.5 us)
Async XLA Ops:
  0.0 99.8 %copy-start = (f32[4,1024]{1,0:T(4,128)S(1)}, f32[4,1024]{1,0:T(4,128)}, u32[]{:S(2)}) copy-start(f32[4,1024]{1,0:T(4,128)} %param.4) | copy-start | bytes 49156
  1.1 7.3 %collective-permute-start = (f32[4,1]{1,0:T(4,128)S(1)}, f32[4,1]{1,0:T(4,128)S(1)}, u32[]{:S(2)}, u32[]{:S(2)}) collective-permute-start(f32[4,1]{1,0:T(4,128)S(1)} %slice.143), channel_id=1, source_target_pairs={{2,0},{4,2},{6,4},{8,6},{10,8},{12,10},{14,12},{16,14},{18,16},{20... | collective-permute-start | bytes 56 | tf_op jit(solution)/shard_map/ppermute | solution.py:12
  8.6 5.5 %collective-permute-start.1 = (f32[4,1]{1,0:T(4,128)S(1)}, f32[4,1]{1,0:T(4,128)S(1)}, u32[]{:S(2)}, u32[]{:S(2)}) collective-permute-start(f32[4,1]{1,0:T(4,128)S(1)} %slice.144), channel_id=1, source_target_pairs={{0,2},{2,4},{4,6},{6,8},{8,10},{10,12},{12,14},{14,16},{16,18},{18... | collective-permute-start | bytes 56 | tf_op jit(solution)/shard_map/ppermute | solution.py:12
  14.7 7.3 %collective-permute-start.2 = (f32[4,1]{1,0:T(4,128)S(1)}, f32[4,1]{1,0:T(4,128)S(1)}, u32[]{:S(2)}, u32[]{:S(2)}) collective-permute-start(f32[4,1]{1,0:T(4,128)S(1)} %slice.147), channel_id=1, source_target_pairs={{2,0},{4,2},{6,4},{8,6},{10,8},{12,10},{14,12},{16,14},{18,16},{20... | collective-permute-start | bytes 56 | tf_op jit(solution)/shard_map/ppermute | solution.py:12
  22.1 5.5 %collective-permute-start.3 = (f32[4,1]{1,0:T(4,128)S(1)}, f32[4,1]{1,0:T(4,128)S(1)}, u32[]{:S(2)}, u32[]{:S(2)}) collective-permute-start(f32[4,1]{1,0:T(4,128)S(1)} %slice.148), channel_id=1, source_target_pairs={{0,2},{2,4},{4,6},{6,8},{8,10},{10,12},{12,14},{14,16},{16,18},{18... | collective-permute-start | bytes 56 | tf_op jit(solution)/shard_map/ppermute | solution.py:12
  28.1 7.3 %collective-permute-start.4 = (f32[4,1]{1,0:T(4,128)S(1)}, f32[4,1]{1,0:T(4,128)S(1)}, u32[]{:S(2)}, u32[]{:S(2)}) collective-permute-start(f32[4,1]{1,0:T(4,128)S(1)} %bitcast.43), channel_id=1, source_target_pairs={{2,0},{4,2},{6,4},{8,6},{10,8},{12,10},{14,12},{16,14},{18,16},{20... | collective-permute-start | bytes 56 | tf_op jit(solution)/shard_map/ppermute | solution.py:12
  35.6 5.5 %collective-permute-start.5 = (f32[4,1]{1,0:T(4,128)S(1)}, f32[4,1]{1,0:T(4,128)S(1)}, u32[]{:S(2)}, u32[]{:S(2)}) collective-permute-start(f32[4,1]{1,0:T(4,128)S(1)} %slice.124), channel_id=1, source_target_pairs={{0,2},{2,4},{4,6},{6,8},{8,10},{10,12},{12,14},{14,16},{16,18},{18... | collective-permute-start | bytes 56 | tf_op jit(solution)/shard_map/ppermute | solution.py:12
  64.1 27.8 %collective-permute-start.10 = (f32[4,1]{1,0:T(4,128)S(1)}, f32[4,1]{1,0:T(4,128)S(1)}, u32[]{:S(2)}, u32[]{:S(2)}) collective-permute-start(f32[4,1]{1,0:T(4,128)S(1)} %get-tuple-element.11), channel_id=1, source_target_pairs={{0,2},{2,4},{4,6},{6,8},{8,10},{10,12},{12,14},{14,16},{16,18},{18... | collective-permute-start | bytes 56 | tf_op jit(solution)/shard_map/ppermute | solution.py:12
  68.3 15.7 %collective-permute-start.8 = (f32[4,1]{1,0:T(4,128)S(1)}, f32[4,1]{1,0:T(4,128)S(1)}, u32[]{:S(2)}, u32[]{:S(2)}) collective-permute-start(f32[4,1]{1,0:T(4,128)S(1)} %get-tuple-element.12), channel_id=1, source_target_pairs={{0,2},{2,4},{4,6},{6,8},{8,10},{10,12},{12,14},{14,16},{16,18},{18... | collective-permute-start | bytes 56 | tf_op jit(solution)/shard_map/ppermute | solution.py:12
  70.8 5.5 %collective-permute-start.6 = (f32[4,1]{1,0:T(4,128)S(1)}, f32[4,1]{1,0:T(4,128)S(1)}, u32[]{:S(2)}, u32[]{:S(2)}) collective-permute-start(f32[4,1]{1,0:T(4,128)S(1)} %get-tuple-element.13), channel_id=1, source_target_pairs={{0,2},{2,4},{4,6},{6,8},{8,10},{10,12},{12,14},{14,16},{16,18},{18... | collective-permute-start | bytes 56 | tf_op jit(solution)/shard_map/ppermute | solution.py:12
  76.4 7.3 %collective-permute-start.7 = (f32[4,1]{1,0:T(4,128)S(1)}, f32[4,1]{1,0:T(4,128)S(1)}, u32[]{:S(2)}, u32[]{:S(2)}) collective-permute-start(f32[4,1]{1,0:T(4,128)S(1)} %bitcast.41), channel_id=1, source_target_pairs={{2,0},{4,2},{6,4},{8,6},{10,8},{12,10},{14,12},{16,14},{18,16},{20... | collective-permute-start | bytes 56 | tf_op jit(solution)/shard_map/ppermute | solution.py:12
  84.2 7.3 %collective-permute-start.9 = (f32[4,1]{1,0:T(4,128)S(1)}, f32[4,1]{1,0:T(4,128)S(1)}, u32[]{:S(2)}, u32[]{:S(2)}) collective-permute-start(f32[4,1]{1,0:T(4,128)S(1)} %slice.158), channel_id=1, source_target_pairs={{2,0},{4,2},{6,4},{8,6},{10,8},{12,10},{14,12},{16,14},{18,16},{20... | collective-permute-start | bytes 56 | tf_op jit(solution)/shard_map/ppermute | solution.py:12
  92.0 7.3 %collective-permute-start.11 = (f32[4,1]{1,0:T(4,128)S(1)}, f32[4,1]{1,0:T(4,128)S(1)}, u32[]{:S(2)}, u32[]{:S(2)}) collective-permute-start(f32[4,1]{1,0:T(4,128)S(1)} %slice.163), channel_id=1, source_target_pairs={{2,0},{4,2},{6,4},{8,6},{10,8},{12,10},{14,12},{16,14},{18,16},{20... | collective-permute-start | bytes 56 | tf_op jit(solution)/shard_map/ppermute | solution.py:12
where the time goes:
time: 101 us; the launch traced here: 100 us
  starting transfers between devices  35.1 us (35%)
  waiting for transfers between devices  34.3 us (34%)
  blocking collectives  16.5 us (16%)
  local copies, waits for them, and re-layouts  6.03 us (6%)
  matrix products  5.94 us (6%)
  other arithmetic  2.4 us (2%)
    ppermute x12, starting transfers between devices, passed_along(): return lax.ppermute(block, axis, route)  35.1 us
    ppermute x12, waiting for transfers between devices, passed_along(): return lax.ppermute(block, axis, route)  34.3 us
    all_to_all x1, blocking collectives, body(): lax.all_to_all(partial_value.reshape(owners, col_blocks, width), 'patch',...  13.1 us
    dot_general x1, matrix products, body(): jnp.einsum('cjkm,crm->cjrk', block_values, blocks, preferred_element_type...  5.63 us
    psum x1, blocking collectives, body(): summed = lax.psum(jnp.sum(arrived, axis=0), 'col')  3.36 us
  transfers between devices with their start and end apart: 12, of which 10 were waited for; matrix products, arithmetic and copies ran while one was open for 4% of the time, Pallas kernels for 0%

commit v1 on v0

v1 whole, which is shorter than its diff:
```python
import functools

import jax
import jax.numpy as jnp
import numpy as np
from jax import lax
from jax.experimental import pallas as pl
from jax.experimental.pallas import tpu as pltpu
from jax.sharding import PartitionSpec as P

LEVELS = 3
LANES = 128
GROUP = 4
MESH = pl.DeviceIdType.MESH


def np_forward(x):
    smooth, details = x, []
    for _ in range(LEVELS):
        even, odd = smooth[:, 0::2], smooth[:, 1::2]
        zero = np.zeros_like(even[:, :1])
        detail = odd - 0.5 * (even + np.concatenate([even[:, 1:], zero], 1))
        smooth = even + 0.25 * (np.concatenate([zero, detail[:, :-1]], 1) + detail)
        details.append(detail)
    return [smooth] + details[::-1]


def np_inverse(pieces):
    smooth = pieces[0]
    for detail in pieces[1:]:
        zero = np.zeros_like(detail[:, :1])
        even = smooth - 0.25 * (np.concatenate([zero, detail[:, :-1]], 1) + detail)
        odd = detail + 0.5 * (even + np.concatenate([even[:, 1:], zero], 1))
        smooth = np.stack([even, odd], -1).reshape(even.shape[0], -1)
    return smooth


def piece_widths(window):
    return [window >> LEVELS] + [window >> level for level in range(LEVELS, 0, -1)]


def forward_matrix(window):
    widths = piece_widths(window)

    def middle(count, at):
        parts = np_forward(np.eye(count * window))
        return np.concatenate([part[:, at * w:(at + 1) * w] for part, w in zip(parts, widths)], 1)

    inner = middle(5, 2)[2 * window - LANES:3 * window + LANES]
    first = middle(5, 0)[:window] - inner[LANES:-LANES]
    last = middle(5, 4)[4 * window:] - inner[LANES:-LANES]
    half = LANES // 2
    result = inner.copy()
    assert not result[:half].any() and not result[-half:].any()
    result[:half] = first[:half]
    result[-half:] = last[-half:]
    assert not first[half:].any() and not last[:-half].any()
    return result


def inverse_matrix(window):
    widths = piece_widths(window)
    count, at = 5, 2
    starts = np.cumsum([0] + widths)

    def response(piece, index):
        pieces = [np.zeros((1, count * w)) for w in widths]
        pieces[piece][0, index] = 1.0
        return np_inverse(pieces)[0, at * window:(at + 1) * window]

    result = np.zeros((3 * window, window))
    for piece, width in enumerate(widths):
        for k in range(width):
            result[starts[piece] + k] = response(piece, at * width + k)
    for piece, width in enumerate(widths):
        if piece:
            result[window + starts[piece] + width - 1] = response(piece, at * width - 1)
        result[window + starts[piece]] += response(piece, (at + 1) * width)
    base = 2 * window
    for row, piece, side in (
        (LANES - 1, 1, -1), (2 * LANES - 1, 2, -1), (2 * LANES - 2, 3, -1),
        (0, 0, 1), (2, 1, 1), (LANES, 2, 1), (1, 3, 1),
    ):
        width = widths[piece]
        result[base + row] = response(piece, at * width - 1 if side < 0 else (at + 1) * width)
    return result


def as_bf16(matrix):
    exact = np.asarray(matrix, dtype=jnp.bfloat16)
    assert (exact.astype(np.float64) == matrix).all()
    return exact


def thirds(value):
    high = value.astype(jnp.bfloat16)
    rest = value - high.astype(jnp.float32)
    middle = rest.astype(jnp.bfloat16)
    low = (rest - middle.astype(jnp.float32)).astype(jnp.bfloat16)
    return jnp.concatenate([high, middle, low], axis=0)


def split_dot(value, matrix):
    rows = value.shape[0]
    out = jnp.dot(thirds(value), matrix, preferred_element_type=jnp.float32)
    return out[:rows] + out[rows:2 * rows] + out[2 * rows:]


def kernel(owners, sides, col_blocks, slots, block, rows_ref, counts_ref, density_ref, values_ref, fwd_ref, inv_ref,
           out_ref, held, fwd, inv, vec, acc, recv, halo, halo_recv, left_in, right_in, mine, other,
           value_sem, fwd_sem, inv_sem, edge_send, edge_recv, send_sem, recv_sem, halo_send_sem, halo_recv_sem, col_sem):
    me = lax.axis_index("patch")
    core = lax.axis_index("col")
    local_len = col_blocks * block
    tall = col_blocks * sides
    groups_per_col = slots // GROUP
    groups = col_blocks * groups_per_col
    windows = local_len // block

    def value_copy(g):
        c = g // groups_per_col
        j = (g % groups_per_col) * GROUP
        return pltpu.make_async_copy(values_ref.at[c, pl.ds(j, GROUP)], held.at[c, pl.ds(j, GROUP)], value_sem.at[g])

    fwd_copy = pltpu.make_async_copy(fwd_ref, fwd, fwd_sem)
    inv_copy = pltpu.make_async_copy(inv_ref, inv, inv_sem)
    fwd_copy.start()

    @pl.loop(0, groups)
    def _(g):
        value_copy(g).start()

    inv_copy.start()

    barrier = pltpu.get_barrier_semaphore()

    @pl.loop(1, owners)
    def _(k):
        pl.semaphore_signal(barrier, inc=1, device_id=(lax.rem(me + k, owners), core), device_id_type=MESH)

    pl.semaphore_signal(barrier, inc=1, device_id=(me, 1 - core), device_id_type=MESH)
    pl.semaphore_wait(barrier, owners)

    to_next = pltpu.make_async_remote_copy(
        src_ref=density_ref.at[:, pl.ds(local_len - LANES, LANES)], dst_ref=left_in,
        send_sem=edge_send.at[0], recv_sem=edge_recv.at[0],
        device_id=(lax.rem(me + 1, owners), core), device_id_type=MESH)
    to_prev = pltpu.make_async_remote_copy(
        src_ref=density_ref.at[:, pl.ds(0, LANES)], dst_ref=right_in,
        send_sem=edge_send.at[1], recv_sem=edge_recv.at[1],
        device_id=(lax.rem(me + owners - 1, owners), core), device_id_type=MESH)

    @pl.when(me < owners - 1)
    def _():
        to_next.start()

    @pl.when(me > 0)
    def _():
        to_prev.start()

    acc[...] = jnp.zeros_like(acc)

    @pl.when(me == 0)
    def _():
        left_in[...] = jnp.zeros_like(left_in)

    @pl.when(me == owners - 1)
    def _():
        right_in[...] = jnp.zeros_like(right_in)

    @pl.when(me > 0)
    def _():
        to_next.wait_recv()

    @pl.when(me < owners - 1)
    def _():
        to_prev.wait_recv()

    lane = lax.broadcasted_iota(jnp.int32, (sides, LANES), 1)
    half = LANES // 2
    density = density_ref[...]
    before = jnp.where(
        lane < half,
        jnp.where(me == 0, density[:, :LANES], 0.0),
        left_in[...])
    after = jnp.where(
        lane >= half,
        jnp.where(me == owners - 1, density[:, local_len - LANES:], 0.0),
        right_in[...])
    rows_in = []
    for w in range(windows):
        start, stop = w * block, (w + 1) * block
        left = before if w == 0 else jnp.where(lane >= half, density[:, start - LANES:start], 0.0)
        right = after if w == windows - 1 else jnp.where(lane < half, density[:, stop:stop + LANES], 0.0)
        rows_in.append(jnp.concatenate([left, density[:, start:stop], right], axis=1))
    fwd_in = jnp.concatenate(rows_in, axis=0)
    fwd_copy.wait()
    lifted = split_dot(fwd_in, fwd[...])
    heads = [lifted[w * sides:(w + 1) * sides, :LANES] for w in range(windows)]
    fine = [lifted[w * sides:(w + 1) * sides, LANES:] for w in range(windows)]

    def turned(value, shift):
        shift = shift % LANES
        return pltpu.roll(value, shift, 1) if shift else value

    quarter = LANES // 4
    smooth = turned(heads[0], 0)
    coarse = turned(heads[0], -quarter)
    for w in range(1, windows):
        inside = lane >= w * quarter
        smooth = jnp.where(inside, turned(heads[w], w * quarter), smooth)
        coarse = jnp.where(inside, turned(heads[w], (w - 1) * quarter), coarse)
    mid = [jnp.where(lane < half, turned(heads[2 * i], half), heads[2 * i + 1]) for i in range(windows // 2)]
    tiles = [smooth, coarse] + mid + fine
    for c in range(col_blocks):
        rounded = jnp.concatenate(tiles[2 * c:2 * c + 2], axis=1).astype(jnp.bfloat16).astype(jnp.float32)
        vec[c] = jnp.concatenate([rounded] * (8 // sides), axis=0)

    height = min(256, acc.shape[0])
    steps = acc.shape[0] // height
    shift = sides.bit_length() - 1
    key = jnp.right_shift(lax.broadcasted_iota(jnp.int32, (height // 8, 8, block), 0) * 8
                          + lax.broadcasted_iota(jnp.int32, (height // 8, 8, block), 1), shift)
    first_slot = core * slots

    def apply_group(g, carry):
        value_copy(g).wait()
        c = g // groups_per_col
        j0 = (g % groups_per_col) * GROUP
        x8 = vec[c]
        targets = []
        for u in range(GROUP):
            alive = first_slot + j0 + u < counts_ref[c]
            targets.append(jnp.where(alive, rows_ref[c, j0 + u], -1))

        def part(step):
            total = acc[pl.ds(step * height, height), :]
            for u in range(GROUP):
                hit = key == targets[u] - step * (height // sides)
                left = jnp.where(hit, x8[None], 0.0).reshape(height, block).astype(jnp.bfloat16)
                total = total + lax.dot_general(left, held[c, j0 + u], (((1,), (1,)), ((), ())),
                                                preferred_element_type=jnp.float32)
            acc[pl.ds(step * height, height), :] = total

        if steps == 1:
            part(0)
        else:
            pl.loop(0, steps)(part)
        return carry

    lax.fori_loop(0, groups, apply_group, 0)

    def main_copy(k, there):
        return pltpu.make_async_remote_copy(
            src_ref=acc.at[pl.ds(there * tall, tall), :], dst_ref=recv.at[me],
            send_sem=send_sem.at[k], recv_sem=recv_sem.at[me],
            device_id=(there, core), device_id_type=MESH)

    def halo_copy(k, there):
        return pltpu.make_async_remote_copy(
            src_ref=halo.at[there], dst_ref=halo_recv.at[me],
            send_sem=halo_send_sem.at[k], recv_sem=halo_recv_sem.at[me],
            device_id=(there, core), device_id_type=MESH)

    @pl.loop(1, owners)
    def _(k):
        main_copy(k, lax.rem(me + k, owners)).start()

    lane8 = lax.broadcasted_iota(jnp.int32, (8, LANES), 1)

    def pack(there):
        prev = acc[pl.ds(jnp.maximum(there - 1, 0) * tall, tall), LANES:]
        nxt = acc[pl.ds(jnp.minimum(there + 1, owners - 1) * tall, tall), :]
        tile = jnp.where(lane8 == LANES - 1, prev[:8], pltpu.roll(prev[8:], LANES - 1, 1))
        tile = jnp.where(lane8 == 0, nxt[:8, :LANES], tile)
        tile = jnp.where(lane8 == 1, pltpu.roll(nxt[8:, :LANES], 1, 1), tile)
        halo[there] = jnp.where(lane8 == 2, pltpu.roll(nxt[:8, LANES:], 2, 1), tile)

    @pl.loop(1, owners)
    def _(k):
        there = lax.rem(me + k, owners)
        pack(there)
        halo_copy(k, there).start()

    pack(me)

    def arrive(k, carry):
        total, edge = carry
        source = lax.rem(me + owners - k, owners)
        pltpu.make_async_remote_copy(
            src_ref=recv.at[source], dst_ref=recv.at[source], send_sem=send_sem.at[k], recv_sem=recv_sem.at[source],
            device_id=(source, core), device_id_type=MESH).wait_recv()
        pltpu.make_async_remote_copy(
            src_ref=halo_recv.at[source], dst_ref=halo_recv.at[source], send_sem=halo_send_sem.at[k],
            recv_sem=halo_recv_sem.at[source], device_id=(source, core), device_id_type=MESH).wait_recv()
        return total + recv[source], edge + halo_recv[source]

    total, edge = lax.fori_loop(
        1, owners, arrive, (acc[pl.ds(me * tall, tall), :], halo[me]))
    mine[:tall] = total
    mine[tall:, :LANES] = edge
    mine[tall:, LANES:] = jnp.zeros_like(edge)
    swap = pltpu.make_async_remote_copy(
        src_ref=mine, dst_ref=other, send_sem=col_sem.at[0], recv_sem=col_sem.at[1],
        device_id=(me, 1 - core), device_id_type=MESH)
    swap.start()

    @pl.loop(1, owners)
    def _(k):
        there = lax.rem(me + k, owners)
        main_copy(k, there).wait_send()
        halo_copy(k, there).wait_send()

    @pl.when(me < owners - 1)
    def _():
        to_next.wait_send()

    @pl.when(me > 0)
    def _():
        to_prev.wait_send()

    inv_copy.wait()
    swap.wait()
    full = mine[...] + other[...]
    total, edge = full[:tall], full[tall:, :LANES]

    def tile(c, side):
        return total[c * sides:(c + 1) * sides, side * LANES:(side + 1) * LANES]

    smooth, coarse = tile(0, 0), tile(0, 1)
    mid = [tile(1, 0), tile(1, 1)]
    fine = [tile(2 + w // 2, w % 2) for w in range(windows)]
    heads = []
    for w in range(windows):
        piece = turned(mid[w // 2], half if w % 2 == 0 else 0)
        piece = jnp.where(lane < half, turned(coarse, quarter - w * quarter), piece)
        heads.append(jnp.where(lane < quarter, turned(smooth, -w * quarter), piece))
    zero = jnp.zeros((sides, LANES), jnp.float32)
    last_tiles = (
        jnp.where(lane == 2, -turned(coarse, 3), jnp.where(lane == 1, -turned(fine[-1], 2), 0.0)),
        jnp.where(lane == 0, -turned(mid[1], 1), 0.0),
    )
    pieces = []
    for w in range(windows):
        head_near = zero
        fine_near = zero
        if w > 0:
            head_near = jnp.where((lane == half - 1) | (lane == LANES - 1), heads[w - 1], head_near)
            fine_near = jnp.where(lane == LANES - 1, fine[w - 1], fine_near)
        if w < windows - 1:
            head_near = jnp.where((lane == 0) | (lane == quarter) | (lane == half), heads[w + 1], head_near)
            fine_near = jnp.where(lane == 0, fine[w + 1], fine_near)
        ends = [zero, zero]
        for i in range(2):
            arrived = edge[i * sides:(i + 1) * sides]
            if w == 0:
                ends[i] = jnp.where((lane >= half) & (me > 0), arrived, ends[i])
            if w == windows - 1:
                ends[i] = jnp.where(lane < half, jnp.where(me == owners - 1, last_tiles[i], arrived), ends[i])
        pieces.append(jnp.concatenate([heads[w], fine[w], head_near, fine_near] + ends, axis=1))
    rebuilt = split_dot(jnp.concatenate(pieces, axis=0), inv[...])
    for w in range(windows):
        at = pl.ds(w * block, block)
        out_ref[:, at] = 0.5 * density_ref[:, at] + rebuilt[w * sides:(w + 1) * sides]


def body(owners, fwd, inv, density, block_values, block_rows, block_counts):
    sides, local_len = density.shape
    col_blocks, slots, block, _ = block_values.shape
    tall = col_blocks * sides
    f32, bf16 = jnp.float32, jnp.bfloat16
    vmem = pl.BlockSpec(memory_space=pltpu.VMEM)
    smem = pl.BlockSpec(memory_space=pltpu.SMEM)
    hbm = pl.BlockSpec(memory_space=pl.ANY)
    dma = pltpu.SemaphoreType.DMA
    return pl.pallas_call(
        functools.partial(kernel, owners, sides, col_blocks, slots, block),
        out_shape=jax.ShapeDtypeStruct(density.shape, f32),
        in_specs=[smem, smem, vmem, hbm, hbm, hbm],
        out_specs=vmem,
        scratch_shapes=[
            pltpu.VMEM(block_values.shape, bf16),
            pltpu.VMEM(fwd.shape, bf16),
            pltpu.VMEM(inv.shape, bf16),
            pltpu.VMEM((col_blocks, 8, block), f32),
            pltpu.VMEM((owners * tall, block), f32),
            pltpu.VMEM((owners, tall, block), f32),
            pltpu.VMEM((owners, 8, LANES), f32),
            pltpu.VMEM((owners, 8, LANES), f32),
            pltpu.VMEM((sides, LANES), f32),
            pltpu.VMEM((sides, LANES), f32),
            pltpu.VMEM((tall + 8, block), f32),
            pltpu.VMEM((tall + 8, block), f32),
            dma((col_blocks * slots // GROUP,)),
            dma, dma, dma((2,)), dma((2,)),
            dma((owners,)), dma((owners,)), dma((owners,)), dma((owners,)),
            dma((2,)),
        ],
        compiler_params=pltpu.CompilerParams(
            collective_id=0, has_side_effects=True, vmem_limit_bytes=60 * 1024 * 1024),
    )(block_rows, block_counts, density, block_values, jnp.asarray(fwd), jnp.asarray(inv))


def solution(mesh):
    owners = mesh.shape["patch"]
    window = 2 * LANES
    fwd, inv = as_bf16(forward_matrix(window)), as_bf16(inverse_matrix(window))
    return jax.shard_map(
        functools.partial(body, owners, fwd, inv),
        mesh=mesh,
        in_specs=(P(None, "patch"), P("patch", "col", None, None), P("patch", "col"), P("patch")),
        out_specs=P(None, "patch"),
        check_vma=False,
    )
```

time: 101 us -> 27.9 us (0.28)
  the two profiles are of different devices: /device:TPU:6 before, /device:TPU:0 now
where the time goes in v1:
time: 27.9 us; the launch traced here: 27.5 us
  Pallas kernels  26.2 us (94%)
  local copies, waits for them, and re-layouts  1.32 us (5%)
    pallas_call x1, Pallas kernels, body(): pl.pallas_call(functools.partial(kernel, owners, sides, col_blocks, slots...  26.2 us
    unnamed x1, local copies, waits for them, and re-layouts  1.32 us

profile of v1, /device:TPU:0, one launch (start us, length us, event | category | flops | bytes accessed | tf_op | source)
XLA Modules:
  0.0 27.5 jit_solution(14616437965586902278)
XLA Ops:
  0.0 26.2 %shard_map.64 = f32[4,1024]{1,0:T(4,128)} custom-call(s32[4,16]{1,0:T(4,128)} %rows_ref.1, s32[4]{0:T(128)} %counts_ref.1, f32[4,1024]{1,0:T(4,128)} %density_ref.1, bf16[4,16,256,256]{3,2,1,0:T(8,128)(2,1)} %values_ref.1, bf16[512,256]{1,0:T(8,128)(2,1)} %constant.4.clone.fwd_ref, bf16[768,256]{1,0:T(8,128)(2,1)} %constant.5.clone.inv_ref), custom_call_target="tpu_custom_call" | custom-call | tf_op jit(solution)/shard_map/pallas_call | solution.py:376
  26.2 1.3 %copy.8 = f32[4,1024]{1,0:T(4,128)} copy(f32[4,1024]{1,0:T(4,128)} %shard_map.64) | data formatting | bytes 32768

commit v2 on v1

--- a/solution.py
+++ b/solution.py
@@ -10,7 +10,7 @@
 
 LEVELS = 3
 LANES = 128
-GROUP = 4
+GROUP = 8
 MESH = pl.DeviceIdType.MESH
 
 
@@ -107,8 +107,8 @@
 
 
 def kernel(owners, sides, col_blocks, slots, block, rows_ref, counts_ref, density_ref, values_ref, fwd_ref, inv_ref,
-           out_ref, held, fwd, inv, vec, acc, recv, halo, halo_recv, left_in, right_in, mine, other,
-           value_sem, fwd_sem, inv_sem, edge_send, edge_recv, send_sem, recv_sem, halo_send_sem, halo_recv_sem, col_sem):
+           out_ref, held, fwd, inv, vec, terms, acc, recv, halo, side_in, left_in, right_in, mine, other,
+           value_sem, fwd_sem, inv_sem, edge_send, edge_recv, send_sem, recv_sem, side_send, side_recv, col_sem):
     me = lax.axis_index("patch")
     core = lax.axis_index("col")
     local_len = col_blocks * block
@@ -126,9 +126,10 @@
     inv_copy = pltpu.make_async_copy(inv_ref, inv, inv_sem)
     fwd_copy.start()
 
-    @pl.loop(0, groups)
-    def _(g):
-        value_copy(g).start()
+    early = col_blocks // 2
+    for c in [early] + [c for c in range(col_blocks) if c != early]:
+        for i in range(groups_per_col):
+            value_copy(c * groups_per_col + i).start()
 
     inv_copy.start()
 
@@ -139,7 +140,10 @@
         pl.semaphore_signal(barrier, inc=1, device_id=(lax.rem(me + k, owners), core), device_id_type=MESH)
 
     pl.semaphore_signal(barrier, inc=1, device_id=(me, 1 - core), device_id_type=MESH)
-    pl.semaphore_wait(barrier, owners)
+
+    for k in (1, owners - 1):
+        pl.semaphore_signal(barrier, inc=1, device_id=(lax.rem(me + k, owners), 1 - core), device_id_type=MESH)
+
 
     to_next = pltpu.make_async_remote_copy(
         src_ref=density_ref.at[:, pl.ds(local_len - LANES, LANES)], dst_ref=left_in,
@@ -150,105 +154,126 @@
         send_sem=edge_send.at[1], recv_sem=edge_recv.at[1],
         device_id=(lax.rem(me + owners - 1, owners), core), device_id_type=MESH)
 
-    @pl.when(me < owners - 1)
-    def _():
-        to_next.start()
-
-    @pl.when(me > 0)
-    def _():
-        to_prev.start()
-
-    acc[...] = jnp.zeros_like(acc)
-
-    @pl.when(me == 0)
-    def _():
-        left_in[...] = jnp.zeros_like(left_in)
-
-    @pl.when(me == owners - 1)
-    def _():
-        right_in[...] = jnp.zeros_like(right_in)
-
-    @pl.when(me > 0)
-    def _():
-        to_next.wait_recv()
-
-    @pl.when(me < owners - 1)
-    def _():
-        to_prev.wait_recv()
-
     lane = lax.broadcasted_iota(jnp.int32, (sides, LANES), 1)
     half = LANES // 2
+    quarter = LANES // 4
     density = density_ref[...]
-    before = jnp.where(
-        lane < half,
-        jnp.where(me == 0, density[:, :LANES], 0.0),
-        left_in[...])
-    after = jnp.where(
-        lane >= half,
-        jnp.where(me == owners - 1, density[:, local_len - LANES:], 0.0),
-        right_in[...])
-    rows_in = []
-    for w in range(windows):
-        start, stop = w * block, (w + 1) * block
-        left = before if w == 0 else jnp.where(lane >= half, density[:, start - LANES:start], 0.0)
-        right = after if w == windows - 1 else jnp.where(lane < half, density[:, stop:stop + LANES], 0.0)
-        rows_in.append(jnp.concatenate([left, density[:, start:stop], right], axis=1))
-    fwd_in = jnp.concatenate(rows_in, axis=0)
-    fwd_copy.wait()
-    lifted = split_dot(fwd_in, fwd[...])
-    heads = [lifted[w * sides:(w + 1) * sides, :LANES] for w in range(windows)]
-    fine = [lifted[w * sides:(w + 1) * sides, LANES:] for w in range(windows)]
 
     def turned(value, shift):
         shift = shift % LANES
         return pltpu.roll(value, shift, 1) if shift else value
 
-    quarter = LANES // 4
-    smooth = turned(heads[0], 0)
-    coarse = turned(heads[0], -quarter)
-    for w in range(1, windows):
-        inside = lane >= w * quarter
-        smooth = jnp.where(inside, turned(heads[w], w * quarter), smooth)
-        coarse = jnp.where(inside, turned(heads[w], (w - 1) * quarter), coarse)
-    mid = [jnp.where(lane < half, turned(heads[2 * i], half), heads[2 * i + 1]) for i in range(windows // 2)]
-    tiles = [smooth, coarse] + mid + fine
+    def lift(from_left, from_right):
+        before = jnp.where(lane < half, jnp.where(me == 0, density[:, :LANES], 0.0), from_left)
+        after = jnp.where(lane >= half, jnp.where(me == owners - 1, density[:, local_len - LANES:], 0.0), from_right)
+        rows_in = []
+        for w in range(windows):
+            start, stop = w * block, (w + 1) * block
+            left = before if w == 0 else jnp.where(lane >= half, density[:, start - LANES:start], 0.0)
+            right = after if w == windows - 1 else jnp.where(lane < half, density[:, stop:stop + LANES], 0.0)
+            rows_in.append(jnp.concatenate([left, density[:, start:stop], right], axis=1))
+        lifted = split_dot(jnp.concatenate(rows_in, axis=0), fwd[...])
+        heads = [lifted[w * sides:(w + 1) * sides, :LANES] for w in range(windows)]
+        fine = [lifted[w * sides:(w + 1) * sides, LANES:] for w in range(windows)]
+        smooth = turned(heads[0], 0)
+        coarse = turned(heads[0], -quarter)
+        for w in range(1, windows):
+            inside = lane >= w * quarter
+            smooth = jnp.where(inside, turned(heads[w], w * quarter), smooth)
+            coarse = jnp.where(inside, turned(heads[w], (w - 1) * quarter), coarse)
+        mid = [jnp.where(lane < half, turned(heads[2 * i], half), heads[2 * i + 1]) for i in range(windows // 2)]
+        return [smooth, coarse] + mid + fine
+
+    def place(tiles, c):
+        column = jnp.concatenate(tiles[2 * c:2 * c + 2], axis=1)
+        vec[c] = jnp.concatenate([column] * (LANES // sides), axis=0).astype(jnp.bfloat16)
+
+    shift = sides.bit_length() - 1
+    lane_slot = jnp.right_shift(lax.broadcasted_iota(jnp.int32, (block, LANES), 1), shift)
+
+    def apply_column(c):
+        at = c * slots * sides
+        here = pl.ds(at // LANES * LANES, LANES)
+        first = at % LANES // sides
+        found = terms[:, here]
+        for i in range(0, groups_per_col):
+            value_copy(c * groups_per_col + i).wait()
+        for i in range(0, slots, GROUP):
+            got = lax.dot_general(held[c, i:i + GROUP].reshape(GROUP * block, block), vec[c],
+                                  (((1,), (1,)), ((), ())), preferred_element_type=jnp.float32)
+            for u in range(GROUP):
+                found = jnp.where(lane_slot == first + i + u, got[u * block:(u + 1) * block], found)
+        terms[:, here] = found
+
+    terms[...] = jnp.zeros_like(terms)
+    fwd_copy.wait()
+    place(lift(jnp.zeros((sides, LANES), jnp.float32), jnp.zeros((sides, LANES), jnp.float32)), early)
+    apply_column(early)
+
+    pl.semaphore_wait(barrier, owners + 2)
+
+    @pl.when(me < owners - 1)
+    def _():
+        to_next.start()
+
+    @pl.when(me > 0)
+    def _():
+        to_prev.start()
+
+    @pl.when(me == 0)
+    def _():
+        left_in[...] = jnp.zeros_like(left_in)
+        side_in[0] = jnp.zeros_like(side_in[0])
+
+    @pl.when(me == owners - 1)
+    def _():
+        right_in[...] = jnp.zeros_like(right_in)
+        side_in[1] = jnp.zeros_like(side_in[1])
+
+    width = terms.shape[1]
+    first_slot = core * slots
+    column_key = lax.broadcasted_iota(jnp.int32, (8, width), 1)
+    column_slot = jnp.right_shift(column_key, shift)
+    wanted = jnp.full((8, width), -1, jnp.int32)
     for c in range(col_blocks):
-        rounded = jnp.concatenate(tiles[2 * c:2 * c + 2], axis=1).astype(jnp.bfloat16).astype(jnp.float32)
-        vec[c] = jnp.concatenate([rounded] * (8 // sides), axis=0)
-
+        count = counts_ref[c]
+        for j in range(slots):
+            row = jnp.where(first_slot + j < count, rows_ref[c, j], -1)
+            wanted = jnp.where(column_slot == c * slots + j, row, wanted)
+    wanted = wanted * sides + jnp.bitwise_and(column_key, sides - 1)
     height = min(256, acc.shape[0])
-    steps = acc.shape[0] // height
-    shift = sides.bit_length() - 1
-    key = jnp.right_shift(lax.broadcasted_iota(jnp.int32, (height // 8, 8, block), 0) * 8
-                          + lax.broadcasted_iota(jnp.int32, (height // 8, 8, block), 1), shift)
-    first_slot = core * slots
-
-    def apply_group(g, carry):
-        value_copy(g).wait()
-        c = g // groups_per_col
-        j0 = (g % groups_per_col) * GROUP
-        x8 = vec[c]
-        targets = []
-        for u in range(GROUP):
-            alive = first_slot + j0 + u < counts_ref[c]
-            targets.append(jnp.where(alive, rows_ref[c, j0 + u], -1))
-
-        def part(step):
-            total = acc[pl.ds(step * height, height), :]
-            for u in range(GROUP):
-                hit = key == targets[u] - step * (height // sides)
-                left = jnp.where(hit, x8[None], 0.0).reshape(height, block).astype(jnp.bfloat16)
-                total = total + lax.dot_general(left, held[c, j0 + u], (((1,), (1,)), ((), ())),
-                                                preferred_element_type=jnp.float32)
-            acc[pl.ds(step * height, height), :] = total
-
-        if steps == 1:
-            part(0)
-        else:
-            pl.loop(0, steps)(part)
-        return carry
-
-    lax.fori_loop(0, groups, apply_group, 0)
+    row_key = (lax.broadcasted_iota(jnp.int32, (height // 8, 8, width), 0) * 8
+               + lax.broadcasted_iota(jnp.int32, (height // 8, 8, width), 1))
+
+    @pl.when(me > 0)
+    def _():
+        to_next.wait_recv()
+
+    @pl.when(me < owners - 1)
+    def _():
+        to_prev.wait_recv()
+
+    tiles = lift(left_in[...], right_in[...])
+    later = [c for c in range(col_blocks) if c != early]
+    for c in later:
+        place(tiles, c)
+    for c in later:
+        apply_column(c)
+
+    split = thirds(terms[...])
+
+    def scatter(step):
+        chosen = jnp.where(row_key == wanted[None] - step * height, 1.0, 0.0).reshape(height, width).astype(jnp.bfloat16)
+        total = jnp.zeros((height, block), jnp.float32)
+        for i in range(3):
+            total = total + lax.dot_general(chosen, split[i * block:(i + 1) * block], (((1,), (1,)), ((), ())),
+                                            preferred_element_type=jnp.float32)
+        acc[pl.ds(step * height, height), :] = total
+
+    if acc.shape[0] == height:
+        scatter(0)
+    else:
+        pl.loop(0, acc.shape[0] // height)(scatter)
 
     def main_copy(k, there):
         return pltpu.make_async_remote_copy(
@@ -256,50 +281,48 @@
             send_sem=send_sem.at[k], recv_sem=recv_sem.at[me],
             device_id=(there, core), device_id_type=MESH)
 
-    def halo_copy(k, there):
-        return pltpu.make_async_remote_copy(
-            src_ref=halo.at[there], dst_ref=halo_recv.at[me],
-            send_sem=halo_send_sem.at[k], recv_sem=halo_recv_sem.at[me],
-            device_id=(there, core), device_id_type=MESH)
+    def side_copies(to_left):
+        side = 1 if to_left else 0
+        there = jnp.maximum(me - 1, 0) if to_left else jnp.minimum(me + 1, owners - 1)
+        return [pltpu.make_async_remote_copy(
+            src_ref=halo, dst_ref=side_in.at[side, core], send_sem=side_send.at[side, to],
+            recv_sem=side_recv.at[side, core], device_id=(there, to), device_id_type=MESH) for to in range(2)]
+
+    def side_arrived(side):
+        for source in range(2):
+            pltpu.make_async_remote_copy(
+                src_ref=halo, dst_ref=side_in.at[side, source], send_sem=side_send.at[side, source],
+                recv_sem=side_recv.at[side, source], device_id=(me, 1 - core), device_id_type=MESH).wait_recv()
 
     @pl.loop(1, owners)
     def _(k):
         main_copy(k, lax.rem(me + k, owners)).start()
 
-    lane8 = lax.broadcasted_iota(jnp.int32, (8, LANES), 1)
-
-    def pack(there):
-        prev = acc[pl.ds(jnp.maximum(there - 1, 0) * tall, tall), LANES:]
-        nxt = acc[pl.ds(jnp.minimum(there + 1, owners - 1) * tall, tall), :]
-        tile = jnp.where(lane8 == LANES - 1, prev[:8], pltpu.roll(prev[8:], LANES - 1, 1))
-        tile = jnp.where(lane8 == 0, nxt[:8, :LANES], tile)
-        tile = jnp.where(lane8 == 1, pltpu.roll(nxt[8:, :LANES], 1, 1), tile)
-        halo[there] = jnp.where(lane8 == 2, pltpu.roll(nxt[:8, LANES:], 2, 1), tile)
-
-    @pl.loop(1, owners)
-    def _(k):
-        there = lax.rem(me + k, owners)
-        pack(there)
-        halo_copy(k, there).start()
-
-    pack(me)
-
-    def arrive(k, carry):
-        total, edge = carry
+    def arrive(k, total):
         source = lax.rem(me + owners - k, owners)
         pltpu.make_async_remote_copy(
             src_ref=recv.at[source], dst_ref=recv.at[source], send_sem=send_sem.at[k], recv_sem=recv_sem.at[source],
             device_id=(source, core), device_id_type=MESH).wait_recv()
-        pltpu.make_async_remote_copy(
-            src_ref=halo_recv.at[source], dst_ref=halo_recv.at[source], send_sem=halo_send_sem.at[k],
-            recv_sem=halo_recv_sem.at[source], device_id=(source, core), device_id_type=MESH).wait_recv()
-        return total + recv[source], edge + halo_recv[source]
-
-    total, edge = lax.fori_loop(
-        1, owners, arrive, (acc[pl.ds(me * tall, tall), :], halo[me]))
-    mine[:tall] = total
-    mine[tall:, :LANES] = edge
-    mine[tall:, LANES:] = jnp.zeros_like(edge)
+        return total + recv[source]
+
+    total = lax.fori_loop(1, owners, arrive, acc[pl.ds(me * tall, tall), :])
+    mine[...] = total
+    lane8 = lax.broadcasted_iota(jnp.int32, (8, LANES), 1)
+    edge = jnp.where(lane8 == LANES - 1, total[:8, LANES:], pltpu.roll(total[8:, LANES:], LANES - 1, 1))
+    edge = jnp.where(lane8 == 0, total[:8, :LANES], edge)
+    edge = jnp.where(lane8 == 1, pltpu.roll(total[8:, :LANES], 1, 1), edge)
+    halo[...] = jnp.where(lane8 == 2, pltpu.roll(total[:8, LANES:], 2, 1), edge)
+
+    @pl.when(me < owners - 1)
+    def _():
+        for copy in side_copies(False):
+            copy.start()
+
+    @pl.when(me > 0)
+    def _():
+        for copy in side_copies(True):
+            copy.start()
+
     swap = pltpu.make_async_remote_copy(
         src_ref=mine, dst_ref=other, send_sem=col_sem.at[0], recv_sem=col_sem.at[1],
         device_id=(me, 1 - core), device_id_type=MESH)
@@ -309,20 +332,32 @@
     def _(k):
         there = lax.rem(me + k, owners)
         main_copy(k, there).wait_send()
-        halo_copy(k, there).wait_send()
 
     @pl.when(me < owners - 1)
     def _():
         to_next.wait_send()
+        for copy in side_copies(False):
+            copy.wait_send()
 
     @pl.when(me > 0)
     def _():
         to_prev.wait_send()
+        for copy in side_copies(True):
+            copy.wait_send()
 
     inv_copy.wait()
     swap.wait()
-    full = mine[...] + other[...]
-    total, edge = full[:tall], full[tall:, :LANES]
+    total = mine[...] + other[...]
+
+    @pl.when(me > 0)
+    def _():
+        side_arrived(0)
+
+    @pl.when(me < owners - 1)
+    def _():
+        side_arrived(1)
+
+    edge = jnp.where(lane8 >= LANES // 2, side_in[0, 0] + side_in[0, 1], side_in[1, 0] + side_in[1, 1])
 
     def tile(c, side):
         return total[c * sides:(c + 1) * sides, side * LANES:(side + 1) * LANES]
@@ -382,18 +417,19 @@
             pltpu.VMEM(block_values.shape, bf16),
             pltpu.VMEM(fwd.shape, bf16),
             pltpu.VMEM(inv.shape, bf16),
-            pltpu.VMEM((col_blocks, 8, block), f32),
+            pltpu.VMEM((col_blocks, LANES, block), bf16),
+            pltpu.VMEM((block, col_blocks * slots * sides), f32),
             pltpu.VMEM((owners * tall, block), f32),
             pltpu.VMEM((owners, tall, block), f32),
-            pltpu.VMEM((owners, 8, LANES), f32),
-            pltpu.VMEM((owners, 8, LANES), f32),
+            pltpu.VMEM((8, LANES), f32),
+            pltpu.VMEM((2, 2, 8, LANES), f32),
             pltpu.VMEM((sides, LANES), f32),
             pltpu.VMEM((sides, LANES), f32),
-            pltpu.VMEM((tall + 8, block), f32),
-            pltpu.VMEM((tall + 8, block), f32),
+            pltpu.VMEM((tall, block), f32),
+            pltpu.VMEM((tall, block), f32),
             dma((col_blocks * slots // GROUP,)),
             dma, dma, dma((2,)), dma((2,)),
-            dma((owners,)), dma((owners,)), dma((owners,)), dma((owners,)),
+            dma((owners,)), dma((owners,)), dma((2, 2)), dma((2, 2)),
             dma((2,)),
         ],
         compiler_params=pltpu.CompilerParams(

time: 27.9 us -> 26.5 us (0.950)
  Pallas kernels: 26.2 us -> 24.8 us
    pallas_call x1, Pallas kernels: 26.2 us -> 24.8 us  [body(): pl.pallas_call(functools.partial(kernel, owners, sides, col_blocks, slots...]
where the time goes in v2:
time: 26.5 us; the launch traced here: 26.1 us
  Pallas kernels  24.8 us (94%)
  local copies, waits for them, and re-layouts  1.32 us (5%)
    pallas_call x1, Pallas kernels, body(): pl.pallas_call(functools.partial(kernel, owners, sides, col_blocks, slots...  24.8 us
    unnamed x1, local copies, waits for them, and re-layouts  1.32 us

profile of v2, /device:TPU:0, one launch (start us, length us, event | category | flops | bytes accessed | tf_op | source)
XLA Modules:
  0.0 26.1 jit_solution(4538329127367433478)
XLA Ops:
  0.0 24.8 %shard_map.64 = f32[4,1024]{1,0:T(4,128)} custom-call(s32[4,16]{1,0:T(4,128)} %rows_ref.1, s32[4]{0:T(128)} %counts_ref.1, f32[4,1024]{1,0:T(4,128)} %density_ref.1, bf16[4,16,256,256]{3,2,1,0:T(8,128)(2,1)} %values_ref.1, bf16[512,256]{1,0:T(8,128)(2,1)} %constant.4.clone.fwd_ref, bf16[768,256]{1,0:T(8,128)(2,1)} %constant.5.clone.inv_ref), custom_call_target="tpu_custom_call" | custom-call | tf_op jit(solution)/shard_map/pallas_call | solution.py:411
  24.8 1.3 %copy.8 = f32[4,1024]{1,0:T(4,128)} copy(f32[4,1024]{1,0:T(4,128)} %shard_map.64) | data formatting | bytes 32768
